TPU v7x, 32 devices: a whole 2x2x4 slice. The times are simulated.
32 devices in a mesh: grp: 2 (over y), slab: 4 (over z), ang: 4 (over x, core).
Axes of the slice: x: 2, y: 2, z: 4, core: 2. Of those that a mesh axis runs over, the one named last changes fastest.
Arguments:
- volume: bfloat16 [16, 256, 1024], P(('grp', 'slab')), parts along dimension 0, may hold values from -6 to 6
- ray_weights: bfloat16 [8, 1024, 1024], P('ang'), may hold values from -0.0625 to 0.0625
- row_offsets: int32 [8, 8], P('ang'), may hold values from 0 to 8
- measured: float32 [16, 256, 1024], P(('grp', 'ang'), 'slab'), parts along dimension 0, may hold values from -6 to 6
- shifts: float32 [16], P(('grp', 'ang')), parts along dimension 0, may hold values from -4 to 4
Outputs:
- updated_volume: bfloat16 [16, 256, 1024], P(('grp', 'slab')), parts along dimension 0
- last_residual: float32 [16, 256, 1024], P(('grp', 'ang'), 'slab'), parts along dimension 0
- shift_slope: float32 [16], P(('grp', 'ang')), parts along dimension 0
There are 2 independent parts, one for each index of `grp`. A program takes and returns all parts, laid end to end along the dimension named above; an argument that names none is the same for every part. Nothing has to cross between parts.
All inputs are finite; a program needn't handle non-finite values.
Results may differ from a plain program's by a relative error of at most 0.006.
Values may be sent and summed in bfloat16 or wider, within the bound.
A program may use at most 128 MiB of HBM per device.

v0:
```python
import math

import jax
import jax.numpy as jnp
from jax import lax
from jax.sharding import PartitionSpec as P

Y = 256
X = 1024
U = 1024
OFF = 8
ROUNDS = 2


step_size = 0.5


def move_down(products, tilt_table):
    base = jnp.zeros((products.shape[1] + OFF, U), jnp.float32)
    placed = jax.vmap(
        lambda block, shift_rows: lax.dynamic_update_slice(base, block, (shift_rows, jnp.int32(0)))
    )(products, tilt_table)
    return jnp.sum(placed, axis=0)


def backproject(extended, tilt_table, ray_weights, band_rows):
    slices_count = tilt_table.shape[1]
    running = jnp.zeros((slices_count * band_rows, X), jnp.float32)
    for angle_index in range(ray_weights.shape[0]):
        source = extended[angle_index]
        picked = jax.vmap(
            lambda shift_rows: lax.dynamic_slice(source, (shift_rows, jnp.int32(0)), (band_rows, U))
        )(tilt_table[angle_index])
        running = running + lax.dot_general(
            picked.reshape(slices_count * band_rows, U),
            ray_weights[angle_index],
            (((1,), (1,)), ((), ())),
            preferred_element_type=jnp.float32,
        )
    return running


def apply_update(current, running):
    partial_value = lax.optimization_barrier(running.reshape(current.shape).astype(jnp.bfloat16))
    partial_wide = partial_value.astype(jnp.float32)
    gradient = lax.psum(partial_wide, "ang")
    renewed = (current.astype(jnp.float32) - step_size * gradient).astype(jnp.bfloat16)
    return renewed


def per_device(volume, ray_weights, row_offsets, measured, shifts):
    angles_here = ray_weights.shape[0]
    band_rows = measured.shape[1]
    highest = lax.Precision.HIGHEST
    numbers = lax.iota(jnp.int32, U)
    turns = numbers[:, None] * numbers[None, :] % U
    radians = turns.astype(jnp.float32) * (2.0 * math.pi / U)
    cosine = jnp.cos(radians)
    sine = jnp.sin(radians)
    signed = jnp.where(numbers <= (U - 1) // 2, numbers, numbers - U)
    omega = signed.astype(jnp.float32) * (2.0 * math.pi / U)
    flat_rows = measured.reshape(angles_here * band_rows, U)
    real_part = jnp.dot(flat_rows, cosine, precision=highest).reshape(angles_here, band_rows, U)
    imag_part = -jnp.dot(flat_rows, sine, precision=highest).reshape(angles_here, band_rows, U)
    phase = omega[None, None, :] * shifts[:, None, None]
    turned_real = real_part * jnp.cos(phase) + imag_part * jnp.sin(phase)
    turned_imag = imag_part * jnp.cos(phase) - real_part * jnp.sin(phase)
    first_half = jnp.concatenate([turned_real, omega * turned_imag], axis=0).reshape(-1, U)
    second_half = jnp.concatenate([turned_imag, -omega * turned_real], axis=0).reshape(-1, U)
    inverse = (
        jnp.dot(first_half, cosine, precision=highest)
        - jnp.dot(second_half, sine, precision=highest)
    ) / U
    inverse = inverse.reshape(2, angles_here, band_rows, U)
    shifted = inverse[0]
    slope_field = inverse[1]
    projection = shifted
    residual = shifted
    current = volume
    slices_here = volume.shape[0]
    tilt_table = lax.dynamic_slice_in_dim(
        row_offsets, lax.axis_index("slab") * slices_here, slices_here, 1
    )
    for round_index in range(ROUNDS):
        flattened = current.reshape(slices_here * Y, X)
        partials = jnp.stack(
            [
                move_down(
                    jnp.dot(
                        flattened, ray_weights[angle_index], preferred_element_type=jnp.float32
                    ).reshape(slices_here, Y, U),
                    tilt_table[angle_index],
                )[:Y]
                for angle_index in range(angles_here)
            ]
        )
        projection = lax.psum_scatter(partials, "slab", scatter_dimension=1, tiled=True)
        residual = projection - shifted
        rounded = residual.astype(jnp.bfloat16)
        gathered = lax.all_gather(rounded, "slab", axis=1, tiled=True)
        extended = jnp.concatenate(
            [gathered, jnp.zeros((angles_here, OFF, U), jnp.bfloat16)], axis=1
        )
        running = backproject(extended, tilt_table, ray_weights, Y)
        current = apply_update(current, running)
    local_dot = jnp.sum(projection * slope_field, axis=(1, 2))
    shift_slope = lax.psum(local_dot, "slab") / math.sqrt(Y * U)
    return (current, residual, shift_slope)


def solution(mesh):
    in_specs = (
        P(("grp", "slab"), None, None),
        P("ang", None, None),
        P("ang", None),
        P(("grp", "ang"), "slab", None),
        P(("grp", "ang")),
    )
    out_specs = (P(("grp", "slab"), None, None), P(("grp", "ang"), "slab", None), P(("grp", "ang")))
    return jax.shard_map(
        per_device, mesh=mesh, in_specs=in_specs, out_specs=out_specs, check_vma=False
    )
```

profile of v0, /device:TPU:1, one launch (start us, length us, event | category | flops | bytes accessed | tf_op | source)
XLA Modules:
  0.0 434.6 jit_solution(13662559025870306911)
XLA Ops:
  7.3 4.6 %fusion.16 = f32[2,256,1024]{2,1,0:T(8,128)} fusion(bf16[2,256,1024]{2,1,0:T(8,128)(2,1)} %param.5, bf16[2,1024,1024]{2,1,0:T(8,128)(2,1)} %param.6), kind=kOutput, calls=%fused_computation.41 | convolution fusion | flops 1073741824 | bytes 5242880 | tf_op jit(solution)/shard_map/dot_general | solution.py:89
  11.9 2.6 fusion.8
  16.4 23.4 %while.12 = (s32[]{:T(128)}, f32[2,264,1024]{2,1,0:T(8,128)}, s32[2,3]{1,0:T(2,128)S(1)}, f32[2,256,1024]{2,1,0:T(8,128)}, s32[]{:T(128)}, /*index=5*/s32[3]{0:T(128)S(1)}, s32[]{:T(128)}) while((s32[]{:T(128)}, f32[2,264,1024]{2,1,0:T(8,128)}, s32[2,3]{1,0:T(2,128)S(1)}, f32[2,256,1024]{2,1,0:T(8,128)}, s32[]{:T(128)}, /*index=5*/s32[3]{0:T(128)S(1)}, ...), condition=%wide.while_cond.4, body=%wide.while_body.4.sunk | while | flops 262163 | bytes 5243051 | solution.py:21
  17.0 2.6 and_reduce_fusion.8
  19.6 3.6 dynamic-slice_select_fusion.8
  23.2 4.9 %dynamic-update-slice.32 = f32[2,264,1024]{2,1,0:T(8,128)} dynamic-update-slice(f32[2,264,1024]{2,1,0:T(8,128)} %get-tuple-element.455, f32[1,256,1024]{2,1,0:T(8,128)S(1)} %dynamic-slice_select_fusion.8, s32[]{:T(128)} %bitcast.154, s32[]{:T(128)} %bitcast.155, s32[]{:T(128)} %constant.18.clone.1..sunk) | dynamic-update-slice | bytes 2097156 | tf_op jit(solution)/shard_map/vmap(vmap())/scatter
  28.7 2.6 and_reduce_fusion.8
  31.3 3.6 dynamic-slice_select_fusion.8
  34.9 4.9 %dynamic-update-slice.32 = f32[2,264,1024]{2,1,0:T(8,128)} dynamic-update-slice(f32[2,264,1024]{2,1,0:T(8,128)} %get-tuple-element.455, f32[1,256,1024]{2,1,0:T(8,128)S(1)} %dynamic-slice_select_fusion.8, s32[]{:T(128)} %bitcast.154, s32[]{:T(128)} %bitcast.155, s32[]{:T(128)} %constant.18.clone.1..sunk) | dynamic-update-slice | bytes 2097156 | tf_op jit(solution)/shard_map/vmap(vmap())/scatter
  41.6 24.2 %while.13 = (s32[]{:T(128)}, f32[2,264,1024]{2,1,0:T(8,128)}, s32[2,3]{1,0:T(2,128)S(1)}, f32[2,256,1024]{2,1,0:T(8,128)}, s32[]{:T(128)}, /*index=5*/s32[3]{0:T(128)S(1)}, s32[]{:T(128)}) while((s32[]{:T(128)}, f32[2,264,1024]{2,1,0:T(8,128)}, s32[2,3]{1,0:T(2,128)S(1)}, f32[2,256,1024]{2,1,0:T(8,128)}, s32[]{:T(128)}, /*index=5*/s32[3]{0:T(128)S(1)}, ...), condition=%wide.while_cond.5, body=%wide.while_body.5.sunk | while | flops 262163 | bytes 5243051 | solution.py:21
  42.2 2.7 and_reduce_fusion.9
  44.9 3.7 dynamic-slice_select_fusion.9
  48.6 5.0 %dynamic-update-slice.33 = f32[2,264,1024]{2,1,0:T(8,128)} dynamic-update-slice(f32[2,264,1024]{2,1,0:T(8,128)} %get-tuple-element.434, f32[1,256,1024]{2,1,0:T(8,128)S(1)} %dynamic-slice_select_fusion.9, s32[]{:T(128)} %bitcast.159, s32[]{:T(128)} %bitcast.160, s32[]{:T(128)} %constant.18.clone.1..sunk.1) | dynamic-update-slice | bytes 2097156 | tf_op jit(solution)/shard_map/vmap(vmap())/scatter
  54.3 2.7 and_reduce_fusion.9
  57.0 3.7 dynamic-slice_select_fusion.9
  60.7 5.0 %dynamic-update-slice.33 = f32[2,264,1024]{2,1,0:T(8,128)} dynamic-update-slice(f32[2,264,1024]{2,1,0:T(8,128)} %get-tuple-element.434, f32[1,256,1024]{2,1,0:T(8,128)S(1)} %dynamic-slice_select_fusion.9, s32[]{:T(128)} %bitcast.159, s32[]{:T(128)} %bitcast.160, s32[]{:T(128)} %constant.18.clone.1..sunk.1) | dynamic-update-slice | bytes 2097156 | tf_op jit(solution)/shard_map/vmap(vmap())/scatter
  65.7 3.0 reduce_sum.45
  73.6 18.6 %fusion.26 = f32[1024,128]{0,1:T(8,128)S(1)} fusion(f32[128,1024]{1,0:T(8,128)S(1)} %bitcast.174), kind=kOutput, calls=%fused_computation.54 | convolution fusion | flops 1625292800 | bytes 1048576 | tf_op jit(solution)/shard_map/dot_general | solution.py:63
  92.2 18.6 %fusion.50 = f32[1024,128]{0,1:T(8,128)S(1)} fusion(f32[128,1024]{1,0:T(8,128)S(1)} %bitcast.175), kind=kOutput, calls=%fused_computation.67 | convolution fusion | flops 1625423872 | bytes 1048576 | tf_op jit(solution)/shard_map/dot_general | solution.py:64
  111.3 20.2 %fusion.24 = f32[256,1024]{1,0:T(8,128)S(1)} fusion(f32[256,1024]{1,0:T(8,128)S(1)} %bitcast.185), kind=kOutput, calls=%fused_computation.53 | convolution fusion | flops 3235905536 | bytes 2097152 | tf_op jit(solution)/shard_map/dot_general | solution.py:71
  131.5 20.1 %fusion.47 = f32[256,1024]{1,0:T(8,128)S(1)} fusion(f32[256,1024]{1,0:T(8,128)S(1)} %fusion.24, f32[256,1024]{1,0:T(8,128)S(1)} %bitcast.184), kind=kOutput, calls=%fused_computation.66 | convolution fusion | flops 3236429824 | bytes 3145728 | tf_op jit(solution)/shard_map/dot_general | solution.py:72
  153.8 29.5 %all-gather.3.cloned.1.call-done = bf16[2,256,1024]{2,1,0:T(8,128)(2,1)} async-done(((bf16[2,64,1024]{2,1,0:T(8,128)(2,1)}), bf16[2,256,1024]{2,1,0:T(8,128)(2,1)}) %all-gather.3.cloned.1.call-update) | async-done | bytes 1048592 | tf_op jit(solution)/shard_map/all_gather | solution.py:100
  185.4 4.2 fusion.10
  190.2 4.5 %add_convert_fusion.1 = bf16[512,1024]{1,0:T(8,128)(2,1)} fusion(f32[512,1024]{1,0:T(8,128)} %fusion.10, bf16[512,1024]{1,0:T(8,128)(2,1)S(1)} %bitcast.182, bf16[2,1024,1024]{2,1,0:T(8,128)(2,1)} %param.6), kind=kOutput, calls=%fused_computation.50 | convolution fusion | flops 1074790400 | bytes 6291456 | tf_op jit(solution)/shard_map/dot_general | solution.py:34
  194.7 42.1 %all-reduce.6 = f32[2,256,1024]{2,1,0:T(8,128)S(1)} all-reduce(bf16[2,256,1024]{2,1,0:T(8,128)(2,1)} %bitcast.178), channel_id=1, replica_groups=mesh['grp'=2,'slab'=4,'ang'=4] {'ang'}, use_global_device_ids=true, to_apply=%region_5.6 | all-reduce | flops 524288 | bytes 3145728 | tf_op jit(solution)/shard_map/psum | solution.py:46
  239.2 2.6 fusion.14
  241.8 2.6 fusion.6
  246.0 23.5 %while.14 = (s32[]{:T(128)}, f32[2,264,1024]{2,1,0:T(8,128)}, s32[2,3]{1,0:T(2,128)S(1)}, f32[2,256,1024]{2,1,0:T(8,128)}, s32[]{:T(128)}, /*index=5*/s32[3]{0:T(128)S(1)}, s32[]{:T(128)}) while((s32[]{:T(128)}, f32[2,264,1024]{2,1,0:T(8,128)}, s32[2,3]{1,0:T(2,128)S(1)}, f32[2,256,1024]{2,1,0:T(8,128)}, s32[]{:T(128)}, /*index=5*/s32[3]{0:T(128)S(1)}, ...), condition=%wide.while_cond.6, body=%wide.while_body.6.sunk | while | flops 262163 | bytes 5243051 | solution.py:21
  246.7 2.6 and_reduce_fusion.10
  249.2 3.5 dynamic-slice_select_fusion.10
  252.8 5.0 %dynamic-update-slice.34 = f32[2,264,1024]{2,1,0:T(8,128)} dynamic-update-slice(f32[2,264,1024]{2,1,0:T(8,128)} %get-tuple-element.527, f32[1,256,1024]{2,1,0:T(8,128)S(1)} %dynamic-slice_select_fusion.10, s32[]{:T(128)} %bitcast.164, s32[]{:T(128)} %bitcast.165, s32[]{:T(128)} %constant.18.clone.1..sunk.2) | dynamic-update-slice | bytes 2097156 | tf_op jit(solution)/shard_map/vmap(vmap())/scatter
  258.4 2.6 and_reduce_fusion.10
  261.0 3.5 dynamic-slice_select_fusion.10
  264.5 5.0 %dynamic-update-slice.34 = f32[2,264,1024]{2,1,0:T(8,128)} dynamic-update-slice(f32[2,264,1024]{2,1,0:T(8,128)} %get-tuple-element.527, f32[1,256,1024]{2,1,0:T(8,128)S(1)} %dynamic-slice_select_fusion.10, s32[]{:T(128)} %bitcast.164, s32[]{:T(128)} %bitcast.165, s32[]{:T(128)} %constant.18.clone.1..sunk.2) | dynamic-update-slice | bytes 2097156 | tf_op jit(solution)/shard_map/vmap(vmap())/scatter
  273.1 23.6 %while.15 = (s32[]{:T(128)}, f32[2,264,1024]{2,1,0:T(8,128)}, s32[2,3]{1,0:T(2,128)S(1)}, f32[2,256,1024]{2,1,0:T(8,128)}, s32[]{:T(128)}, /*index=5*/s32[3]{0:T(128)S(1)}, s32[]{:T(128)}) while((s32[]{:T(128)}, f32[2,264,1024]{2,1,0:T(8,128)}, s32[2,3]{1,0:T(2,128)S(1)}, f32[2,256,1024]{2,1,0:T(8,128)}, s32[]{:T(128)}, /*index=5*/s32[3]{0:T(128)S(1)}, ...), condition=%wide.while_cond.7, body=%wide.while_body.7.sunk | while | flops 262163 | bytes 5243051 | solution.py:21
  273.7 2.6 and_reduce_fusion.11
  276.3 3.6 dynamic-slice_select_fusion.11
  279.9 5.0 %dynamic-update-slice.35 = f32[2,264,1024]{2,1,0:T(8,128)} dynamic-update-slice(f32[2,264,1024]{2,1,0:T(8,128)} %get-tuple-element.506, f32[1,256,1024]{2,1,0:T(8,128)S(1)} %dynamic-slice_select_fusion.11, s32[]{:T(128)} %bitcast.169, s32[]{:T(128)} %bitcast.170, s32[]{:T(128)} %constant.18.clone.1..sunk.3) | dynamic-update-slice | bytes 2097156 | tf_op jit(solution)/shard_map/vmap(vmap())/scatter
  285.5 2.6 and_reduce_fusion.11
  288.1 3.6 dynamic-slice_select_fusion.11
  291.7 5.0 %dynamic-update-slice.35 = f32[2,264,1024]{2,1,0:T(8,128)} dynamic-update-slice(f32[2,264,1024]{2,1,0:T(8,128)} %get-tuple-element.506, f32[1,256,1024]{2,1,0:T(8,128)S(1)} %dynamic-slice_select_fusion.11, s32[]{:T(128)} %bitcast.169, s32[]{:T(128)} %bitcast.170, s32[]{:T(128)} %constant.18.clone.1..sunk.3) | dynamic-update-slice | bytes 2097156 | tf_op jit(solution)/shard_map/vmap(vmap())/scatter
  300.3 42.1 %reduce-scatter.5.cloned.1.call-done = f32[2,64,1024]{2,1,0:T(8,128)} async-done(((f32[2,256,1024]{2,1,0:T(8,128)}), f32[2,64,1024]{2,1,0:T(8,128)}) %reduce-scatter.5.cloned.1.call-update) | async-done | bytes 524304 | tf_op jit(solution)/shard_map/reduce_scatter | solution.py:97
  344.5 8.7 %psum.23 = f32[2]{0:T(128)S(1)} all-reduce(f32[2]{0:T(128)S(1)} %get-tuple-element.189), channel_id=1, replica_groups=mesh['grp'=2,'slab'=4,'ang'=4] {'slab'}, use_global_device_ids=true, to_apply=%region_13.14 | all-reduce | flops 2 | bytes 16 | tf_op jit(solution)/shard_map/psum | solution.py:107
  353.7 18.1 %all-gather.5.cloned.1.call-done = bf16[2,256,1024]{2,1,0:T(8,128)(2,1)} async-done(((bf16[2,64,1024]{2,1,0:T(8,128)(2,1)}), bf16[2,256,1024]{2,1,0:T(8,128)(2,1)}) %all-gather.5.cloned.1.call-update) | async-done | bytes 1048592 | tf_op jit(solution)/shard_map/all_gather | solution.py:100
  373.6 4.2 fusion.12
  378.4 4.5 %add_convert_fusion = bf16[512,1024]{1,0:T(8,128)(2,1)} fusion(f32[512,1024]{1,0:T(8,128)} %fusion.12, bf16[512,1024]{1,0:T(8,128)(2,1)S(1)} %bitcast.180, bf16[2,1024,1024]{2,1,0:T(8,128)(2,1)} %param.6), kind=kOutput, calls=%fused_computation.48 | convolution fusion | flops 1074790400 | bytes 6291456 | tf_op jit(solution)/shard_map/dot_general | solution.py:34
  382.9 42.2 %all-reduce.7 = f32[2,256,1024]{2,1,0:T(8,128)S(1)} all-reduce(bf16[2,256,1024]{2,1,0:T(8,128)(2,1)} %bitcast.179), channel_id=1, replica_groups=mesh['grp'=2,'slab'=4,'ang'=4] {'ang'}, use_global_device_ids=true, to_apply=%region_11.12 | all-reduce | flops 524288 | bytes 3145728 | tf_op jit(solution)/shard_map/psum | solution.py:46
  425.1 2.6 subtract_convert_fusion
  (106 shorter events, 36.4 us)
Async XLA Ops:
  7.2 66.5 %copy-start = (f32[2,64,1024]{2,1,0:T(8,128)S(1)}, f32[2,64,1024]{2,1,0:T(8,128)}, u32[]{:S(2)}) copy-start(f32[2,64,1024]{2,1,0:T(8,128)} %param.8) | copy-start | bytes 1572868
  7.2 144.6 %reduce-scatter.3.cloned.1.call-start = ((), (), s32[]{:S(2)}) async-start(), calls=%async_computation.2 | async-start | bytes 2621440 | tf_op jit(solution)/shard_map/reduce_scatter | solution.py:97
  7.2 4.7 %copy-start.4 = (bf16[2,256,1024]{2,1,0:T(8,128)(2,1)S(1)}, bf16[2,256,1024]{2,1,0:T(8,128)(2,1)}, u32[]{:S(2)}) copy-start(bf16[2,256,1024]{2,1,0:T(8,128)(2,1)} %param.5) | copy-start | bytes 3145732
  7.2 4.7 %copy-start.9 = (bf16[2,1024,1024]{2,1,0:T(8,128)(2,1)S(1)}, bf16[2,1024,1024]{2,1,0:T(8,128)(2,1)}, u32[]{:S(2)}) copy-start(bf16[2,1024,1024]{2,1,0:T(8,128)(2,1)} %param.6) | copy-start | bytes 12582916
  11.9 2.6 copy-start.6
  11.9 2.7 copy-start.7
  14.5 1.9 copy-start.5
  65.7 3.0 copy-start.2
  71.7 1.7 copy-start.8
  73.2 110.2 %all-gather.3.cloned.1.call-start = ((), (), s32[]{:S(2)}) async-start(), calls=%async_computation.3 | async-start | bytes 1310720 | tf_op jit(solution)/shard_map/all_gather | solution.py:100
  153.6 188.8 %reduce-scatter.5.cloned.1.call-start = ((), (), s32[]{:S(2)}) async-start(), calls=%async_computation.4 | async-start | bytes 2621440 | tf_op jit(solution)/shard_map/reduce_scatter | solution.py:97
  236.7 2.5 copy-start.10
  239.2 2.6 copy-start.3
  300.2 71.6 %all-gather.5.cloned.1.call-start = ((), (), s32[]{:S(2)}) async-start(), calls=%async_computation.5 | async-start | bytes 1310720 | tf_op jit(solution)/shard_map/all_gather | solution.py:100
  382.9 44.7 %copy-start.1 = (f32[2,64,1024]{2,1,0:T(8,128)S(1)}, f32[2,64,1024]{2,1,0:T(8,128)}, u32[]{:S(2)}) copy-start(f32[2,64,1024]{2,1,0:T(8,128)} %param.8) | copy-start | bytes 1572868
Sparse Core Ops, SparseCore 0:
  73.3 45.3 reduce-scatter.2
  153.7 29.5 all-gather.2
  300.3 42.0 reduce-scatter.4
  344.7 27.0 all-gather.4
where the time goes:
time: 440 us; the launch traced here: 435 us
  matrix products  107 us (24%)
  blocking collectives  92.9 us (21%)
  waiting for transfers between devices  89.8 us (20%)
  other arithmetic  70.2 us (16%)
  local copies, waits for them, and re-layouts  59 us (13%)
  between operations  14.5 us (3%)
    psum x2, blocking collectives, apply_update(): gradient = lax.psum(partial_wide, 'ang')  84.2 us
    scatter x16, other arithmetic  49.8 us
    all_gather x2, waiting for transfers between devices, per_device(): gathered = lax.all_gather(rounded, 'slab', axis=1, tiled=True)  47.6 us
    scatter x24, local copies, waits for them, and re-layouts  44.8 us
    reduce_scatter x2, waiting for transfers between devices, per_device(): lax.psum_scatter(partials, 'slab', scatter_dimension=1, tiled=True)  42.2 us
    dot_general x1, matrix products, per_device(): jnp.dot(first_half, cosine, precision=highest)  20.2 us
    dot_general x1, matrix products, per_device(): jnp.dot(second_half, sine, precision=highest)  20.1 us
    dot_general x1, matrix products, per_device(): jnp.dot(flat_rows, sine, precision=highest)  18.6 us
  transfers between devices with their start and end apart: 4, of which 3 were waited for; matrix products, arithmetic and copies ran while one was open for 18% of the time, Pallas kernels for 0%

commit v1 on v0

--- a/solution.py
+++ b/solution.py
@@ -1,8 +1,13 @@
 import math
+
+import functools
 
 import jax
 import jax.numpy as jnp
+import numpy as np
 from jax import lax
+from jax.experimental import pallas as pl
+from jax.experimental.pallas import tpu as pltpu
 from jax.sharding import PartitionSpec as P
 
 Y = 256
@@ -108,7 +113,401 @@
     return (current, residual, shift_slope)
 
 
+F32 = jnp.float32
+BF16 = jnp.bfloat16
+HALO = 16
+FINE = 32
+
+
+def wave_tables(columns):
+    half = columns // 2
+    k = np.arange(half)[None, :]
+    coarse = np.arange(columns // FINE)[:, None] * FINE
+    fine = np.arange(FINE)[:, None]
+    turn = 2.0 * np.pi / columns
+    coarse_turns = (coarse * k % columns) * turn
+    fine_turns = (fine * k % columns) * turn
+    fine_sine = np.sin(fine_turns)
+    fine_sine[:, 0] = 1.0 - 2.0 * (np.arange(FINE) % 2)
+    tables = (np.cos(coarse_turns), np.sin(coarse_turns), np.cos(fine_turns), fine_sine)
+    return [jnp.asarray(t.astype(np.float32)) for t in tables]
+
+
+def split(value):
+    high = value.astype(BF16)
+    return high, (value - high.astype(F32)).astype(BF16)
+
+
+def dot(a, b):
+    return jnp.dot(a, b, preferred_element_type=F32)
+
+
+def dot_t(a, b):
+    return lax.dot_general(a, b, (((1,), (1,)), ((), ())), preferred_element_type=F32)
+
+
+def fit_kernel(
+    n, m, off, shifts, vol, w_hbm, meas, ctab, stab, ftab, gtab,
+    out, res_out, slope_out,
+    w, wave_hi, wave_lo, spec, wide, field, db, dh, ub, band, halo, acc, ext,
+    psend, precv, own, xsend, xrecv, fresh, sl,
+    w_sem, loc_sem, zs, zr, ags, agr, rhs, rhr, ps, pr, xs, xr, hs, hr, fs, fr, os_, or_, ss, sr,
+):
+    slab = lax.axis_index("slab")
+    me = lax.axis_index("ang")
+    angles, rows, cols = meas.shape
+    slices = vol.shape[0]
+    nz = slices * n
+    qc = vol.shape[2] // m
+    mate = me + 1 - 2 * (me % 2)
+    across = (me + 2) % m
+    diagonal = (mate + 2) % m
+    later = (slab + 1) % n
+    earlier = (slab + n - 1) % n
+
+    def remote(src, dst, send, recv, **where):
+        return pltpu.make_async_remote_copy(
+            src_ref=src, dst_ref=dst, send_sem=send, recv_sem=recv,
+            device_id=where, device_id_type=pl.DeviceIdType.MESH,
+        )
+
+    w_copy = pltpu.make_async_copy(w_hbm, w, w_sem)
+    w_copy.start()
+    barrier = pltpu.get_barrier_semaphore()
+    for hop in range(1, n):
+        pl.semaphore_signal(
+            barrier, 1, device_id={"slab": (slab + hop) % n}, device_id_type=pl.DeviceIdType.MESH
+        )
+    for peer in (mate, across):
+        pl.semaphore_signal(barrier, 1, device_id={"ang": peer}, device_id_type=pl.DeviceIdType.MESH)
+    pl.semaphore_wait(barrier, n + 1)
+
+    def quarter(q):
+        return pl.ds(pl.multiple_of(q * qc, qc), qc)
+
+    def band_rows(d):
+        return pl.ds(pl.multiple_of(d * rows, rows), rows)
+
+    def halo_rows(d):
+        return pl.ds(pl.multiple_of((d + n - 1) % n * rows + rows - HALO, HALO), HALO)
+
+    mine = pl.ds(slab * slices, slices)
+    first = []
+    for hop in range(1, n):
+        d = (slab + hop) % n
+        first.append(remote(vol.at[:, band_rows(d), quarter(me)], band.at[0, me, mine],
+                            zs.at[hop - 1], zr.at[hop - 1], slab=d))
+        first.append(remote(vol.at[:, halo_rows(d), quarter(me)], halo.at[0, me, mine],
+                            zs.at[n - 2 + hop], zr.at[n - 2 + hop], slab=d))
+    for copy in first:
+        copy.start()
+    local = [
+        pltpu.make_async_copy(vol.at[:, band_rows(slab), quarter(me)], band.at[0, me, mine], loc_sem.at[0]),
+        pltpu.make_async_copy(vol.at[:, halo_rows(slab), quarter(me)], halo.at[0, me, mine], loc_sem.at[1]),
+    ]
+    for copy in local:
+        copy.start()
+
+    half = cols // 2
+
+    def wave_rows(i, carry):
+        at = pl.ds(pl.multiple_of(i * FINE, FINE), FINE)
+        cc, cs = ctab[pl.ds(i, 1), :], stab[pl.ds(i, 1), :]
+        fc, fs_ = ftab[...], gtab[...]
+        hi, lo = split(cc * fc - cs * fs_)
+        wave_hi[at, :half] = hi
+        wave_lo[at, :half] = lo
+        hi, lo = split(cs * fc + cc * fs_)
+        wave_hi[at, half:] = hi
+        wave_lo[at, half:] = lo
+        return carry
+
+    lax.fori_loop(0, cols // FINE, wave_rows, 0)
+    flat = angles * rows
+    x_hi, x_lo = split(meas[...].reshape(flat, cols))
+    wide[:flat, :] = x_hi
+    wide[flat : 2 * flat, :] = x_lo
+    tile = 256
+
+    def forward(j, carry):
+        at = pl.ds(pl.multiple_of(j * tile, tile), tile)
+        both = dot(wide[: 2 * flat, :], wave_hi[:, at])
+        spec[:, at] = both[:flat] + both[flat:] + dot(wide[:flat, :], wave_lo[:, at])
+        return carry
+
+    lax.fori_loop(0, cols // tile, forward, 0)
+
+    def gather_start(t, kind, buf, q):
+        return [
+            remote(buf.at[t, q], buf.at[t, q], ags.at[t, kind, 0], agr.at[t, kind, 0], ang=across),
+            remote(buf.at[t, q], buf.at[t, q], ags.at[t, kind, 1], agr.at[t, kind, 1], ang=mate),
+            remote(buf.at[t, across], buf.at[t, across], ags.at[t, kind, 2], agr.at[t, kind, 2], ang=mate),
+        ]
+
+    for copy in first:
+        copy.wait()
+    for copy in local:
+        copy.wait()
+    gathers = [gather_start(0, 0, band, me), gather_start(0, 1, halo, me)]
+    for gather in gathers:
+        gather[0].start()
+        gather[1].start()
+
+    column = lax.broadcasted_iota(jnp.int32, (1, half), 1)
+    base = column == 0
+    omega = column.astype(F32) * (2.0 * math.pi / cols)
+    turn_rate = jnp.where(base, math.pi, omega)
+    weight = jnp.where(base, 1.0 / cols, 2.0 / cols)
+    for a in range(angles):
+        phase = turn_rate * shifts[a]
+        cn, sn = jnp.cos(phase), jnp.sin(phase)
+        cr = jnp.where(base, 1.0, cn)
+        sr_ = jnp.where(base, 0.0, sn)
+        re = spec[a * rows : (a + 1) * rows, :half]
+        im = spec[a * rows : (a + 1) * rows, half:]
+        parts = (
+            (re * cr - im * sr_) * weight,
+            (im * cn + re * sr_) * weight,
+            (im * cr + re * sr_) * (-omega * weight),
+            re * (omega * weight * cr) - im * (turn_rate * weight * sn),
+        )
+        for which in range(2):
+            at = (which * angles + a) * rows
+            for side in range(2):
+                hi, lo = split(parts[2 * which + side])
+                wide[at : at + rows, side * half : (side + 1) * half] = hi
+                wide[2 * flat + at : 2 * flat + at + rows, side * half : (side + 1) * half] = lo
+
+    def backward(j, carry):
+        at = pl.ds(pl.multiple_of(j * tile, tile), tile)
+        both = dot_t(wide[...], wave_hi[at, :])
+        field[:, at] = both[: 2 * flat] + both[2 * flat :] + dot_t(wide[: 2 * flat, :], wave_lo[at, :])
+        return carry
+
+    lax.fori_loop(0, cols // tile, backward, 0)
+
+    for depth, target in ((rows, db), (HALO, dh)):
+        row = lax.broadcasted_iota(jnp.int32, (rows, nz * depth), 0)
+        col = lax.broadcasted_iota(jnp.int32, (rows, nz * depth), 1)
+        for a in range(angles):
+            moved = row - col % depth
+            for z in range(nz):
+                moved = jnp.where(col // depth == z, moved - off[a, z], moved)
+            if target is dh:
+                moved = moved + HALO
+                hit = jnp.where(moved == 0, jnp.where(slab > 0, 1.0, 0.0), 0.0)
+            else:
+                hit = jnp.where(moved == 0, 1.0, 0.0)
+            target[a * rows : (a + 1) * rows, :] = hit.astype(BF16)
+
+    tall_rows = rows + HALO
+    row = lax.broadcasted_iota(jnp.int32, (rows, 2 * angles * tall_rows), 0)
+    col = lax.broadcasted_iota(jnp.int32, (rows, 2 * angles * tall_rows), 1)
+    for z in range(nz):
+        moved = col % tall_rows - row
+        for a in range(angles):
+            moved = jnp.where(col // tall_rows % angles == a, moved - off[a, z], moved)
+        ub[z * rows : (z + 1) * rows, :] = jnp.where(moved == 0, 1.0, 0.0).astype(BF16)
+
+    w_copy.wait()
+
+    def project(t, q, fresh_sum):
+        moved = dot(db[...], band[t, q].reshape(nz * rows, qc)) + dot(dh[...], halo[t, q].reshape(nz * HALO, qc))
+        hi, lo = split(moved)
+        for a in range(angles):
+            both = jnp.concatenate([hi[a * rows : (a + 1) * rows], lo[a * rows : (a + 1) * rows]], axis=0)
+            part = dot(both, w[a, quarter(q), :])
+            acc[a] = part if fresh_sum else acc[a] + part
+
+    def spread(q, store):
+        backs = [split(dot_t(ext_now[a], w[a, quarter(q), :])) for a in range(angles)]
+        tall = jnp.concatenate([hi for hi, _ in backs] + [lo for _, lo in backs], axis=0)
+        store(dot(ub[...], tall).astype(BF16).reshape(nz, rows, qc))
+
+    pending = []
+    for t in range(ROUNDS):
+        last = t == ROUNDS - 1
+        project(t, me, True) if t == 0 else None
+        if t > 0:
+            halo_copy.wait()
+            gathers.append(gather_start(t, 1, halo, me))
+            gathers[1][0].start()
+            gathers[1][1].start()
+            project(t, me, True)
+        for gather in gathers:
+            gather[0].wait_recv()
+            gather[2].start()
+        project(t, across, False)
+        for gather in gathers:
+            gather[1].wait_recv()
+        project(t, mate, False)
+        for gather in gathers:
+            gather[2].wait_recv()
+        project(t, diagonal, False)
+        for gather in gathers:
+            pending.extend(gather)
+        ext_now = ext.at[t]
+        for a in range(angles):
+            projection = acc[a, :rows, :] + acc[a, rows:, :]
+            residual = projection - field[a * rows : (a + 1) * rows, :]
+            ext_now[a, :rows, :] = residual.astype(BF16)
+            if last:
+                res_out[a] = residual
+                slope = field[(angles + a) * rows : (angles + a + 1) * rows, :]
+                line = jnp.sum(projection * slope, axis=0, keepdims=True)
+                sl[0, pl.ds(a, 1), :] = line
+        edge = remote(ext_now.at[:, :HALO, :], ext_now.at[:, pl.ds(rows, HALO), :], rhs.at[t], rhr.at[t], slab=earlier)
+        edge.start()
+        if last:
+            slopes = []
+            for hop in range(1, n):
+                slopes.append(remote(sl.at[0], sl.at[hop], ss.at[hop - 1], sr.at[hop - 1], slab=(slab + hop) % n))
+                slopes[-1].start()
+        edge.wait()
+        keep = jnp.where(slab < n - 1, 1.0, 0.0)
+        for a in range(angles):
+            ext_now[a, rows:, :] = (ext_now[a, rows:, :].astype(F32) * keep).astype(BF16)
+
+        sends = []
+        for slot, q in ((0, diagonal), (1, mate)):
+            def put(value, slot=slot):
+                psend[t, slot] = value
+            spread(q, put)
+            copy = remote(psend.at[t, slot], precv.at[t, slot], ps.at[t, slot], pr.at[t, slot], ang=mate)
+            copy.start()
+            sends.append(copy)
+
+        def put_own(value):
+            own[...] = value
+
+        spread(across, put_own)
+        sends[0].wait_recv()
+        xsend[t] = (own[...].astype(F32) + precv[t, 0].astype(F32)).astype(BF16)
+        x_copy = remote(xsend.at[t], xrecv.at[t], xs.at[t], xr.at[t], ang=across)
+        x_copy.start()
+        spread(me, put_own)
+        sends[1].wait_recv()
+        x_copy.wait_recv()
+        pending.extend(sends)
+        pending.append(x_copy)
+        gradient = own[...].astype(F32) + precv[t, 1].astype(F32) + xrecv[t].astype(F32)
+        renewed = (band[t, me].astype(F32) - step_size * gradient).astype(BF16)
+        if last:
+            fresh[...] = renewed
+        else:
+            band[t + 1, me] = renewed
+            halo_copy = remote(
+                band.at[t + 1, me, :, pl.ds(rows - HALO, HALO), :], halo.at[t + 1, me], hs.at[t], hr.at[t], slab=later
+            )
+            halo_copy.start()
+            gathers = [gather_start(t + 1, 0, band, me)]
+            gathers[0][0].start()
+            gathers[0][1].start()
+
+    finals = []
+    for hop in range(1, n):
+        d = (slab + hop) % n
+        finals.append(remote(fresh.at[pl.ds(d * slices, slices)], out.at[:, band_rows(slab), quarter(me)],
+                             fs.at[hop - 1], fr.at[hop - 1], slab=d))
+        finals[-1].start()
+    keep_own = pltpu.make_async_copy(fresh.at[mine], out.at[:, band_rows(slab), quarter(me)], loc_sem.at[2])
+    keep_own.start()
+    for copy in slopes:
+        copy.wait_recv()
+    total = sl[0]
+    for hop in range(1, n):
+        total = total + sl[hop]
+    slope_out[...] = jnp.broadcast_to(
+        jnp.sum(total, axis=1, keepdims=True) * (1.0 / math.sqrt(rows * n * cols)), slope_out.shape
+    )
+    for copy in finals:
+        copy.wait_recv()
+    keep_own.wait()
+    mine_out = out.at[:, :, quarter(me)]
+    across_out = out.at[:, :, quarter(across)]
+    ends = [
+        remote(mine_out, mine_out, os_.at[0], or_.at[0], ang=across),
+        remote(mine_out, mine_out, os_.at[1], or_.at[1], ang=mate),
+        remote(across_out, across_out, os_.at[2], or_.at[2], ang=mate),
+    ]
+    ends[0].start()
+    ends[1].start()
+    ends[0].wait_recv()
+    ends[2].start()
+    ends[1].wait_recv()
+    ends[2].wait_recv()
+    for copy in pending + slopes + finals + ends:
+        copy.wait_send()
+
+
+def fused(n, m, volume, ray_weights, row_offsets, measured, shifts):
+    angles, rows, cols = measured.shape
+    slices, _, xcells = volume.shape
+    nz = slices * n
+    qc = xcells // m
+    flat = angles * rows
+    quad = (nz, rows, qc)
+    dma = pltpu.SemaphoreType.DMA
+    vmem = pl.BlockSpec(memory_space=pltpu.VMEM)
+    smem = pl.BlockSpec(memory_space=pltpu.SMEM)
+    current, residual, slope = pl.pallas_call(
+        functools.partial(fit_kernel, n, m),
+        name="fit",
+        out_shape=(
+            jax.ShapeDtypeStruct(volume.shape, BF16),
+            jax.ShapeDtypeStruct(measured.shape, F32),
+            jax.ShapeDtypeStruct((angles, 128), F32),
+        ),
+        in_specs=[smem, smem, vmem, pl.BlockSpec(memory_space=pl.ANY), vmem] + [vmem] * 4,
+        out_specs=(vmem, vmem, vmem),
+        scratch_shapes=[
+            pltpu.VMEM(ray_weights.shape, BF16),
+            pltpu.VMEM((cols, cols), BF16),
+            pltpu.VMEM((cols, cols), BF16),
+            pltpu.VMEM((flat, cols), F32),
+            pltpu.VMEM((4 * flat, cols), BF16),
+            pltpu.VMEM((2 * flat, cols), F32),
+            pltpu.VMEM((flat, nz * rows), BF16),
+            pltpu.VMEM((flat, nz * HALO), BF16),
+            pltpu.VMEM((nz * rows, 2 * angles * (rows + HALO)), BF16),
+            pltpu.VMEM((ROUNDS, m) + quad, BF16),
+            pltpu.VMEM((ROUNDS, m, nz, HALO, qc), BF16),
+            pltpu.VMEM((angles, 2 * rows, cols), F32),
+            pltpu.VMEM((ROUNDS, angles, rows + HALO, cols), BF16),
+            pltpu.VMEM((ROUNDS, 2) + quad, BF16),
+            pltpu.VMEM((ROUNDS, 2) + quad, BF16),
+            pltpu.VMEM(quad, BF16),
+            pltpu.VMEM((ROUNDS,) + quad, BF16),
+            pltpu.VMEM((ROUNDS,) + quad, BF16),
+            pltpu.VMEM(quad, BF16),
+            pltpu.VMEM((n, angles, cols), F32),
+            dma, dma((3,)),
+            dma((2 * n - 2,)), dma((2 * n - 2,)),
+            dma((ROUNDS, 2, 3)), dma((ROUNDS, 2, 3)),
+            dma((ROUNDS,)), dma((ROUNDS,)),
+            dma((ROUNDS, 2)), dma((ROUNDS, 2)),
+            dma((ROUNDS,)), dma((ROUNDS,)),
+            dma((ROUNDS,)), dma((ROUNDS,)),
+            dma((n - 1,)), dma((n - 1,)),
+            dma((3,)), dma((3,)),
+            dma((n - 1,)), dma((n - 1,)),
+        ],
+        compiler_params=pltpu.CompilerParams(
+            collective_id=0, has_side_effects=True, vmem_limit_bytes=60 * 1024 * 1024
+        ),
+    )(row_offsets, shifts, volume, ray_weights, measured, *wave_tables(cols))
+    return current, residual, slope[:, 0]
+
+
+def step(n, m, volume, ray_weights, row_offsets, measured, shifts):
+    band_rows = measured.shape[1]
+    if m == 4 and n > 1 and band_rows % HALO == 0 and OFF <= HALO:
+        return fused(n, m, volume, ray_weights, row_offsets, measured, shifts)
+    return per_device(volume, ray_weights, row_offsets, measured, shifts)
+
+
 def solution(mesh):
+    local = functools.partial(step, mesh.shape["slab"], mesh.shape["ang"])
     in_specs = (
         P(("grp", "slab"), None, None),
         P("ang", None, None),
@@ -118,5 +517,5 @@
     )
     out_specs = (P(("grp", "slab"), None, None), P(("grp", "ang"), "slab", None), P(("grp", "ang")))
     return jax.shard_map(
-        per_device, mesh=mesh, in_specs=in_specs, out_specs=out_specs, check_vma=False
+        local, mesh=mesh, in_specs=in_specs, out_specs=out_specs, check_vma=False
     )

time: 440 us -> 82.3 us (0.19); the launches traced: 435 us -> 81.9 us
  matrix products: 107 us -> 0 us
  blocking collectives: 92.9 us -> 0 us
  waiting for transfers between devices: 89.8 us -> 0 us
  Pallas kernels: 0 us -> 75.9 us
  other arithmetic: 70.2 us -> 0 us
  local copies, waits for them, and re-layouts: 59 us -> 5.43 us
  between operations: 14.5 us -> 0.64 us
    dot_general x12 -> x0, matrix products: 107 us -> none  [the longest x1 20.2 us: per_device(): jnp.dot(first_half, cosine, precision=highest)]
    psum x3 -> x0, blocking collectives: 92.9 us -> none  [the longest x2 84.2 us: apply_update(): gradient = lax.psum(partial_wide, 'ang')]
    pallas_call x0 -> x1, Pallas kernels: none -> 75.9 us  [fused(): pl.pallas_call(functools.partial(fit_kernel, n, m), name='fit', out_shape...]
    scatter x17 -> x0, other arithmetic: 49.8 us -> none
    all_gather x2 -> x0, waiting for transfers between devices: 47.6 us -> none  [per_device(): gathered = lax.all_gather(rounded, 'slab', axis=1, tiled=True)]
    scatter x24 -> x0, local copies, waits for them, and re-layouts: 44.8 us -> none
    reduce_scatter x2 -> x0, waiting for transfers between devices: 42.2 us -> none  [per_device(): lax.psum_scatter(partials, 'slab', scatter_dimension=1, tiled=True)]
    another operation x7 -> x0, local copies, waits for them, and re-layouts: 8.38 us -> none
  transfers between devices with their start and end apart: 4 -> 0, of which waited for: 3 -> 0; matrix products, arithmetic and copies ran while one was open for 18% -> 0% of each run, Pallas kernels for 0% -> 0%
where the time goes in v1:
time: 82.3 us; the launch traced here: 81.9 us
  Pallas kernels  75.9 us (92%)
  local copies, waits for them, and re-layouts  5.43 us (7%)
    pallas_call x1, Pallas kernels, fused(): pl.pallas_call(functools.partial(fit_kernel, n, m), name='fit', out_shape...  75.9 us
    unnamed x2, local copies, waits for them, and re-layouts  4.15 us

profile of v1, /device:TPU:1, one launch (start us, length us, event | category | flops | bytes accessed | tf_op | source)
XLA Modules:
  0.0 81.9 jit_solution(5946395597075180060)
XLA Ops:
  0.6 75.9 %fit.1 = (bf16[2,256,1024]{2,1,0:T(8,128)(2,1)}, f32[2,64,1024]{2,1,0:T(8,128)}, f32[2,128]{1,0:T(2,128)}) custom-call(s32[2,8]{1,0:T(2,128)} %off.1, f32[2]{0:T(128)} %shifts.1, bf16[2,256,1024]{2,1,0:T(8,128)(2,1)} %vol.1, bf16[2,1024,1024]{2,1,0:T(8,128)(2,1)} %w_hbm.1, f32[2,64,1024]{2,1,0:T(8,128)} %meas.1, f32[32,512]{1,0:T(8,128)} %constant.8.clone.ctab, ...), custom_call_target="tpu_custom_call" | custom-call | tf_op jit(solution)/shard_map/fit/pallas_call | solution.py:453
  76.5 1.3 %slice_reduce_fusion = f32[2]{0:T(128)} fusion(f32[2,128]{1,0:T(2,128)} %get-tuple-element.8), kind=kLoop, calls=%fused_computation | loop fusion | bytes 16 | tf_op jit(solution)/shard_map/slice | solution.py:499
  77.8 2.3 %copy.14 = bf16[2,256,1024]{2,1,0:T(8,128)(2,1)} copy(bf16[2,256,1024]{2,1,0:T(8,128)(2,1)} %get-tuple-element.12) | data formatting | bytes 2097152
  80.1 1.9 %copy.15 = f32[2,64,1024]{2,1,0:T(8,128)} copy(f32[2,64,1024]{2,1,0:T(8,128)} %get-tuple-element.13) | data formatting | bytes 1048576

commit v2 on v1

--- a/solution.py
+++ b/solution.py
@@ -151,7 +151,7 @@
     out, res_out, slope_out,
     w, wave_hi, wave_lo, spec, wide, field, db, dh, ub, band, halo, acc, ext,
     psend, precv, own, xsend, xrecv, fresh, sl,
-    w_sem, loc_sem, zs, zr, ags, agr, rhs, rhr, ps, pr, xs, xr, hs, hr, fs, fr, os_, or_, ss, sr,
+    w_sem, loc_sem, zs, zr, gs, gr, ags, agr, rhs, rhr, ps, pr, xs, xr, cs, cr_, hs, hr, fs, fr, os_, or_, ss, sr,
 ):
     slab = lax.axis_index("slab")
     me = lax.axis_index("ang")
@@ -201,10 +201,11 @@
                             zs.at[n - 2 + hop], zr.at[n - 2 + hop], slab=d))
     for copy in first:
         copy.start()
-    local = [
-        pltpu.make_async_copy(vol.at[:, band_rows(slab), quarter(me)], band.at[0, me, mine], loc_sem.at[0]),
-        pltpu.make_async_copy(vol.at[:, halo_rows(slab), quarter(me)], halo.at[0, me, mine], loc_sem.at[1]),
-    ]
+    local = []
+    for q in range(m):
+        columns = pl.ds(q * qc, qc)
+        local.append(pltpu.make_async_copy(vol.at[:, band_rows(slab), columns], band.at[0, q, mine], loc_sem.at[2 * q]))
+        local.append(pltpu.make_async_copy(vol.at[:, halo_rows(slab), columns], halo.at[0, q, mine], loc_sem.at[2 * q + 1]))
     for copy in local:
         copy.start()
 
@@ -237,21 +238,49 @@
 
     lax.fori_loop(0, cols // tile, forward, 0)
 
-    def gather_start(t, kind, buf, q):
-        return [
-            remote(buf.at[t, q], buf.at[t, q], ags.at[t, kind, 0], agr.at[t, kind, 0], ang=across),
-            remote(buf.at[t, q], buf.at[t, q], ags.at[t, kind, 1], agr.at[t, kind, 1], ang=mate),
-            remote(buf.at[t, across], buf.at[t, across], ags.at[t, kind, 2], agr.at[t, kind, 2], ang=mate),
-        ]
-
-    for copy in first:
-        copy.wait()
-    for copy in local:
-        copy.wait()
-    gathers = [gather_start(0, 0, band, me), gather_start(0, 1, halo, me)]
-    for gather in gathers:
-        gather[0].start()
-        gather[1].start()
+    def pieces(hop):
+        source = pl.ds((slab + n - hop) % n * slices, slices)
+        steps = []
+        for stage, (q, peer) in enumerate(((me, across), (me, mate), (across, mate))):
+            for kind, buf in enumerate((band, halo)):
+                ref = buf.at[0, q, source]
+                at = (kind, stage, hop - 1)
+                steps.append(remote(ref, ref, gs.at[at], gr.at[at], ang=peer))
+        return steps
+
+    passing = {}
+
+    def pass_on(hop):
+        first[2 * hop - 2].wait_recv()
+        first[2 * hop - 1].wait_recv()
+        passing[hop] = pieces(hop)
+        for copy in passing[hop][:4]:
+            copy.start()
+
+    pass_on(1)
+
+    for depth, target in ((rows, db), (HALO, dh)):
+        row = lax.broadcasted_iota(jnp.int32, (rows, nz * depth), 0)
+        col = lax.broadcasted_iota(jnp.int32, (rows, nz * depth), 1)
+        for a in range(angles):
+            moved = row - col % depth
+            for z in range(nz):
+                moved = jnp.where(col // depth == z, moved - off[a, z], moved)
+            if target is dh:
+                moved = moved + HALO
+                hit = jnp.where(moved == 0, jnp.where(slab > 0, 1.0, 0.0), 0.0)
+            else:
+                hit = jnp.where(moved == 0, 1.0, 0.0)
+            target[a * rows : (a + 1) * rows, :] = hit.astype(BF16)
+
+    tall_rows = rows + HALO
+    row = lax.broadcasted_iota(jnp.int32, (rows, 2 * angles * tall_rows), 0)
+    col = lax.broadcasted_iota(jnp.int32, (rows, 2 * angles * tall_rows), 1)
+    for z in range(nz):
+        moved = col % tall_rows - row
+        for a in range(angles):
+            moved = jnp.where(col // tall_rows % angles == a, moved - off[a, z], moved)
+        ub[z * rows : (z + 1) * rows, :] = jnp.where(moved == 0, 1.0, 0.0).astype(BF16)
 
     column = lax.broadcasted_iota(jnp.int32, (1, half), 1)
     base = column == 0
@@ -278,6 +307,9 @@
                 wide[at : at + rows, side * half : (side + 1) * half] = hi
                 wide[2 * flat + at : 2 * flat + at + rows, side * half : (side + 1) * half] = lo
 
+    for hop in range(2, n):
+        pass_on(hop)
+
     def backward(j, carry):
         at = pl.ds(pl.multiple_of(j * tile, tile), tile)
         both = dot_t(wide[...], wave_hi[at, :])
@@ -286,29 +318,19 @@
 
     lax.fori_loop(0, cols // tile, backward, 0)
 
-    for depth, target in ((rows, db), (HALO, dh)):
-        row = lax.broadcasted_iota(jnp.int32, (rows, nz * depth), 0)
-        col = lax.broadcasted_iota(jnp.int32, (rows, nz * depth), 1)
-        for a in range(angles):
-            moved = row - col % depth
-            for z in range(nz):
-                moved = jnp.where(col // depth == z, moved - off[a, z], moved)
-            if target is dh:
-                moved = moved + HALO
-                hit = jnp.where(moved == 0, jnp.where(slab > 0, 1.0, 0.0), 0.0)
-            else:
-                hit = jnp.where(moved == 0, 1.0, 0.0)
-            target[a * rows : (a + 1) * rows, :] = hit.astype(BF16)
-
-    tall_rows = rows + HALO
-    row = lax.broadcasted_iota(jnp.int32, (rows, 2 * angles * tall_rows), 0)
-    col = lax.broadcasted_iota(jnp.int32, (rows, 2 * angles * tall_rows), 1)
-    for z in range(nz):
-        moved = col % tall_rows - row
-        for a in range(angles):
-            moved = jnp.where(col // tall_rows % angles == a, moved - off[a, z], moved)
-        ub[z * rows : (z + 1) * rows, :] = jnp.where(moved == 0, 1.0, 0.0).astype(BF16)
-
+    pending = list(first)
+    for copy in local:
+        copy.wait()
+    for hop in range(1, n):
+        for copy in passing[hop][:2]:
+            copy.wait_recv()
+        for copy in passing[hop][4:]:
+            copy.start()
+        pending.extend(passing[hop])
+    zero_halo = jnp.zeros((nz, HALO, qc), BF16)
+    for t in range(1, ROUNDS):
+        halo[t, me] = zero_halo
+        halo[t, across] = zero_halo
     w_copy.wait()
 
     def project(t, q, fresh_sum):
@@ -324,28 +346,29 @@
         tall = jnp.concatenate([hi for hi, _ in backs] + [lo for _, lo in backs], axis=0)
         store(dot(ub[...], tall).astype(BF16).reshape(nz, rows, qc))
 
-    pending = []
+    upper = pl.ds(0, rows - HALO)
+    lower = pl.ds(rows - HALO, HALO)
     for t in range(ROUNDS):
         last = t == ROUNDS - 1
-        project(t, me, True) if t == 0 else None
-        if t > 0:
-            halo_copy.wait()
-            gathers.append(gather_start(t, 1, halo, me))
-            gathers[1][0].start()
-            gathers[1][1].start()
+        if t == 0:
             project(t, me, True)
-        for gather in gathers:
-            gather[0].wait_recv()
-            gather[2].start()
-        project(t, across, False)
-        for gather in gathers:
-            gather[1].wait_recv()
-        project(t, mate, False)
-        for gather in gathers:
-            gather[2].wait_recv()
-        project(t, diagonal, False)
-        for gather in gathers:
-            pending.extend(gather)
+            for hop in range(1, n):
+                for copy in passing[hop][2:4]:
+                    copy.wait_recv()
+            project(t, mate, False)
+            project(t, across, False)
+            for hop in range(1, n):
+                for copy in passing[hop][4:]:
+                    copy.wait_recv()
+            project(t, diagonal, False)
+        else:
+            shares[0].wait_recv()
+            shares[2].wait_recv()
+            project(t, mate, False)
+            project(t, across, False)
+            shares[1].wait_recv()
+            shares[3].wait_recv()
+            project(t, diagonal, False)
         ext_now = ext.at[t]
         for a in range(angles):
             projection = acc[a, :rows, :] + acc[a, rows:, :]
@@ -357,61 +380,143 @@
                 line = jnp.sum(projection * slope, axis=0, keepdims=True)
                 sl[0, pl.ds(a, 1), :] = line
         edge = remote(ext_now.at[:, :HALO, :], ext_now.at[:, pl.ds(rows, HALO), :], rhs.at[t], rhr.at[t], slab=earlier)
-        edge.start()
+
+        @pl.when(slab > 0)
+        def _():
+            edge.start()
+
         if last:
             slopes = []
             for hop in range(1, n):
                 slopes.append(remote(sl.at[0], sl.at[hop], ss.at[hop - 1], sr.at[hop - 1], slab=(slab + hop) % n))
                 slopes[-1].start()
-        edge.wait()
-        keep = jnp.where(slab < n - 1, 1.0, 0.0)
-        for a in range(angles):
-            ext_now[a, rows:, :] = (ext_now[a, rows:, :].astype(F32) * keep).astype(BF16)
-
-        sends = []
-        for slot, q in ((0, diagonal), (1, mate)):
-            def put(value, slot=slot):
-                psend[t, slot] = value
-            spread(q, put)
-            copy = remote(psend.at[t, slot], precv.at[t, slot], ps.at[t, slot], pr.at[t, slot], ang=mate)
-            copy.start()
-            sends.append(copy)
-
-        def put_own(value):
-            own[...] = value
-
-        spread(across, put_own)
+
+        @pl.when(slab < n - 1)
+        def _():
+            edge.wait_recv()
+
+        @pl.when(slab == n - 1)
+        def _():
+            ext_now[:, rows:, :] = jnp.zeros((angles, HALO, cols), BF16)
+
+        def put(ref):
+            def store(value):
+                ref[...] = value
+            return store
+
+        sends = [
+            remote(psend.at[t, slot], precv.at[t, slot], ps.at[t, slot], pr.at[t, slot], ang=mate)
+            for slot in range(2)
+        ]
+        pending.extend(sends)
+
+        def x_copy(half_, part, rows_):
+            at = (t, 2 * half_ + part)
+            return remote(xsend.at[t, half_, :, rows_, :], xrecv.at[t, half_, :, rows_, :], xs.at[at], xr.at[at], ang=across)
+
+        spread(diagonal, put(psend.at[t, 0]))
+        sends[0].start()
+        spread(across, put(own))
         sends[0].wait_recv()
-        xsend[t] = (own[...].astype(F32) + precv[t, 0].astype(F32)).astype(BF16)
-        x_copy = remote(xsend.at[t], xrecv.at[t], xs.at[t], xr.at[t], ang=across)
-        x_copy.start()
-        spread(me, put_own)
+        xsend[t, 0] = (own[...].astype(F32) + precv[t, 0].astype(F32)).astype(BF16)
+        if last:
+            chunks = []
+            for hop in list(range(1, n)) + [0]:
+                to = pl.ds((slab + hop) % n * slices, slices)
+                chunks.append((hop, to, remote(xsend.at[t, 0, to], xrecv.at[t, 0, to], cs.at[hop], cr_.at[hop], ang=across)))
+                chunks[-1][2].start()
+                pending.append(chunks[-1][2])
+        else:
+            x_copies = [x_copy(0, 0, lower), x_copy(0, 1, upper)]
+            x_copies[0].start()
+            x_copies[1].start()
+        spread(mate, put(psend.at[t, 1]))
+        sends[1].start()
+        spread(me, put(own))
         sends[1].wait_recv()
-        x_copy.wait_recv()
-        pending.extend(sends)
-        pending.append(x_copy)
-        gradient = own[...].astype(F32) + precv[t, 1].astype(F32) + xrecv[t].astype(F32)
-        renewed = (band[t, me].astype(F32) - step_size * gradient).astype(BF16)
-        if last:
-            fresh[...] = renewed
+        if not last:
+            xsend[t, 1] = (own[...].astype(F32) + precv[t, 1].astype(F32)).astype(BF16)
+            x_copies += [x_copy(1, 0, lower), x_copy(1, 1, upper)]
+            x_copies[2].start()
+            x_copies[3].start()
+            pending.extend(x_copies)
+            shares = []
+            halos = []
+            for k, q in enumerate((me, across)):
+                ref = band.at[t + 1, q]
+                shares.append(remote(ref, ref, ags.at[t, k], agr.at[t, k], ang=mate))
+                halos.append(remote(band.at[t + 1, q, :, lower, :], halo.at[t + 1, q], hs.at[t, k], hr.at[t, k], slab=later))
+            for k, q in enumerate((me, across)):
+                ref = halo.at[t + 1, q]
+                shares.append(remote(ref, ref, ags.at[t, 2 + k], agr.at[t, 2 + k], ang=mate))
+            pending.extend(shares)
+
+            def renew(k, q, rows_):
+                gradient = xsend[t, 1 - k, :, rows_, :].astype(F32) + xrecv[t, k, :, rows_, :].astype(F32)
+                kept = band[t, q, :, rows_, :].astype(F32)
+                band[t + 1, q, :, rows_, :] = (kept - step_size * gradient).astype(BF16)
+
+            def halo_start(k):
+                @pl.when(slab < n - 1)
+                def _():
+                    halos[k].start()
+
+            def halo_take(k):
+                @pl.when(slab > 0)
+                def _():
+                    halos[k].wait_recv()
+
+                shares[2 + k].start()
+
+            x_copies[0].wait_recv()
+            renew(0, me, lower)
+            halo_start(0)
+            x_copies[1].wait_recv()
+            renew(0, me, upper)
+            shares[0].start()
+            x_copies[2].wait_recv()
+            renew(1, across, lower)
+            halo_start(1)
+            halo_take(0)
+            project(t + 1, me, True)
+            x_copies[3].wait_recv()
+            renew(1, across, upper)
+            shares[1].start()
+            halo_take(1)
+
+            @pl.when(slab < n - 1)
+            def _():
+                halos[0].wait_send()
+                halos[1].wait_send()
+
+        @pl.when(slab > 0)
+        def _():
+            edge.wait_send()
+
+    def out_steps(hop):
+        e = (slab + n - hop) % n
+        steps = []
+        for stage, (q, peer) in enumerate(((me, across), (me, mate), (across, mate))):
+            ref = out.at[:, band_rows(e), quarter(q)]
+            steps.append(remote(ref, ref, os_.at[stage, hop], or_.at[stage, hop], ang=peer))
+        return steps
+
+    finals = []
+    t = ROUNDS - 1
+    for hop, to, chunk in chunks:
+        chunk.wait_recv()
+        gradient = own[to].astype(F32) + precv[t, 1, to].astype(F32) + xrecv[t, 0, to].astype(F32)
+        renewed = (band[t, me, to].astype(F32) - step_size * gradient).astype(BF16)
+        if hop:
+            fresh[to] = renewed
+            finals.append(remote(fresh.at[to], out.at[:, band_rows(slab), quarter(me)],
+                                 fs.at[hop - 1], fr.at[hop - 1], slab=(slab + hop) % n))
+            finals[-1].start()
         else:
-            band[t + 1, me] = renewed
-            halo_copy = remote(
-                band.at[t + 1, me, :, pl.ds(rows - HALO, HALO), :], halo.at[t + 1, me], hs.at[t], hr.at[t], slab=later
-            )
-            halo_copy.start()
-            gathers = [gather_start(t + 1, 0, band, me)]
-            gathers[0][0].start()
-            gathers[0][1].start()
-
-    finals = []
-    for hop in range(1, n):
-        d = (slab + hop) % n
-        finals.append(remote(fresh.at[pl.ds(d * slices, slices)], out.at[:, band_rows(slab), quarter(me)],
-                             fs.at[hop - 1], fr.at[hop - 1], slab=d))
-        finals[-1].start()
-    keep_own = pltpu.make_async_copy(fresh.at[mine], out.at[:, band_rows(slab), quarter(me)], loc_sem.at[2])
-    keep_own.start()
+            out[:, band_rows(slab), quarter(me)] = renewed
+    ends = [out_steps(hop) for hop in range(n)]
+    ends[0][0].start()
+    ends[0][1].start()
     for copy in slopes:
         copy.wait_recv()
     total = sl[0]
@@ -420,23 +525,18 @@
     slope_out[...] = jnp.broadcast_to(
         jnp.sum(total, axis=1, keepdims=True) * (1.0 / math.sqrt(rows * n * cols)), slope_out.shape
     )
-    for copy in finals:
-        copy.wait_recv()
-    keep_own.wait()
-    mine_out = out.at[:, :, quarter(me)]
-    across_out = out.at[:, :, quarter(across)]
-    ends = [
-        remote(mine_out, mine_out, os_.at[0], or_.at[0], ang=across),
-        remote(mine_out, mine_out, os_.at[1], or_.at[1], ang=mate),
-        remote(across_out, across_out, os_.at[2], or_.at[2], ang=mate),
-    ]
-    ends[0].start()
-    ends[1].start()
-    ends[0].wait_recv()
-    ends[2].start()
-    ends[1].wait_recv()
-    ends[2].wait_recv()
-    for copy in pending + slopes + finals + ends:
+    for hop in range(1, n):
+        finals[hop - 1].wait_recv()
+        ends[hop][0].start()
+        ends[hop][1].start()
+    for steps in ends:
+        steps[0].wait_recv()
+        steps[2].start()
+    for steps in ends:
+        steps[1].wait_recv()
+        steps[2].wait_recv()
+        pending.extend(steps)
+    for copy in pending + slopes + finals:
         copy.wait_send()
 
 
@@ -477,19 +577,21 @@
             pltpu.VMEM((ROUNDS, 2) + quad, BF16),
             pltpu.VMEM((ROUNDS, 2) + quad, BF16),
             pltpu.VMEM(quad, BF16),
-            pltpu.VMEM((ROUNDS,) + quad, BF16),
-            pltpu.VMEM((ROUNDS,) + quad, BF16),
+            pltpu.VMEM((ROUNDS, 2) + quad, BF16),
+            pltpu.VMEM((ROUNDS, 2) + quad, BF16),
             pltpu.VMEM(quad, BF16),
             pltpu.VMEM((n, angles, cols), F32),
-            dma, dma((3,)),
+            dma, dma((2 * m,)),
             dma((2 * n - 2,)), dma((2 * n - 2,)),
-            dma((ROUNDS, 2, 3)), dma((ROUNDS, 2, 3)),
+            dma((2, 3, n - 1)), dma((2, 3, n - 1)),
+            dma((ROUNDS, 4)), dma((ROUNDS, 4)),
             dma((ROUNDS,)), dma((ROUNDS,)),
             dma((ROUNDS, 2)), dma((ROUNDS, 2)),
-            dma((ROUNDS,)), dma((ROUNDS,)),
-            dma((ROUNDS,)), dma((ROUNDS,)),
+            dma((ROUNDS, 4)), dma((ROUNDS, 4)),
+            dma((n,)), dma((n,)),
+            dma((ROUNDS, 2)), dma((ROUNDS, 2)),
             dma((n - 1,)), dma((n - 1,)),
-            dma((3,)), dma((3,)),
+            dma((3, n)), dma((3, n)),
             dma((n - 1,)), dma((n - 1,)),
         ],
         compiler_params=pltpu.CompilerParams(

time: 82.3 us -> 71.9 us (0.87); the launches traced: 81.9 us -> 70.7 us
  Pallas kernels: 75.9 us -> 64.6 us
    pallas_call x1, Pallas kernels: 75.9 us -> 64.6 us  [fused(): pl.pallas_call(functools.partial(fit_kernel, n, m), name='fit', out_shape...]
where the time goes in v2:
time: 71.9 us; the launch traced here: 70.7 us
  Pallas kernels  64.6 us (90%)
  local copies, waits for them, and re-layouts  5.43 us (8%)
    pallas_call x1, Pallas kernels, fused(): pl.pallas_call(functools.partial(fit_kernel, n, m), name='fit', out_shape...  64.6 us
    unnamed x2, local copies, waits for them, and re-layouts  4.15 us

profile of v2, /device:TPU:1, one launch (start us, length us, event | category | flops | bytes accessed | tf_op | source)
XLA Modules:
  0.0 70.7 jit_solution(5195522306078505650)
XLA Ops:
  0.6 64.6 %fit.1 = (bf16[2,256,1024]{2,1,0:T(8,128)(2,1)}, f32[2,64,1024]{2,1,0:T(8,128)}, f32[2,128]{1,0:T(2,128)}) custom-call(s32[2,8]{1,0:T(2,128)} %off.1, f32[2]{0:T(128)} %shifts.1, bf16[2,256,1024]{2,1,0:T(8,128)(2,1)} %vol.1, bf16[2,1024,1024]{2,1,0:T(8,128)(2,1)} %w_hbm.1, f32[2,64,1024]{2,1,0:T(8,128)} %meas.1, f32[32,512]{1,0:T(8,128)} %constant.8.clone.ctab, ...), custom_call_target="tpu_custom_call" | custom-call | tf_op jit(solution)/shard_map/fit/pallas_call | solution.py:553
  65.2 1.3 %slice_reduce_fusion = f32[2]{0:T(128)} fusion(f32[2,128]{1,0:T(2,128)} %get-tuple-element.8), kind=kLoop, calls=%fused_computation | loop fusion | bytes 16 | tf_op jit(solution)/shard_map/slice | solution.py:601
  66.5 2.3 %copy.14 = bf16[2,256,1024]{2,1,0:T(8,128)(2,1)} copy(bf16[2,256,1024]{2,1,0:T(8,128)(2,1)} %get-tuple-element.12) | data formatting | bytes 2097152
  68.8 1.9 %copy.15 = f32[2,64,1024]{2,1,0:T(8,128)} copy(f32[2,64,1024]{2,1,0:T(8,128)} %get-tuple-element.13) | data formatting | bytes 1048576

commit v3 on v2

--- a/solution.py
+++ b/solution.py
@@ -540,6 +540,19 @@
         copy.wait_send()
 
 
+def place_kernel(current, residual, slope, current_out, residual_out, slope_out, sem_a, sem_b):
+    copies = (
+        pltpu.make_async_copy(current, current_out, sem_a),
+        pltpu.make_async_copy(residual, residual_out, sem_b),
+    )
+    for copy in copies:
+        copy.start()
+    for a in range(slope.shape[0]):
+        slope_out[a] = slope[a, 0]
+    for copy in copies:
+        copy.wait()
+
+
 def fused(n, m, volume, ray_weights, row_offsets, measured, shifts):
     angles, rows, cols = measured.shape
     slices, _, xcells = volume.shape
@@ -558,7 +571,7 @@
             jax.ShapeDtypeStruct(measured.shape, F32),
             jax.ShapeDtypeStruct((angles, 128), F32),
         ),
-        in_specs=[smem, smem, vmem, pl.BlockSpec(memory_space=pl.ANY), vmem] + [vmem] * 4,
+        in_specs=[smem, smem, vmem, pl.BlockSpec(memory_space=pltpu.HBM), vmem] + [vmem] * 4,
         out_specs=(vmem, vmem, vmem),
         scratch_shapes=[
             pltpu.VMEM(ray_weights.shape, BF16),
@@ -595,10 +608,23 @@
             dma((n - 1,)), dma((n - 1,)),
         ],
         compiler_params=pltpu.CompilerParams(
-            collective_id=0, has_side_effects=True, vmem_limit_bytes=60 * 1024 * 1024
+            collective_id=0, has_side_effects=True, vmem_limit_bytes=36 * 1024 * 1024
         ),
     )(row_offsets, shifts, volume, ray_weights, measured, *wave_tables(cols))
-    return current, residual, slope[:, 0]
+    hbm = pl.BlockSpec(memory_space=pl.ANY)
+    return pl.pallas_call(
+        place_kernel,
+        name="place",
+        out_shape=(
+            jax.ShapeDtypeStruct(volume.shape, BF16),
+            jax.ShapeDtypeStruct(measured.shape, F32),
+            jax.ShapeDtypeStruct((angles,), F32),
+        ),
+        in_specs=[vmem, vmem, vmem],
+        out_specs=(hbm, hbm, smem),
+        scratch_shapes=[dma, dma],
+        compiler_params=pltpu.CompilerParams(vmem_limit_bytes=8 * 1024 * 1024),
+    )(current, residual, slope)
 
 
 def step(n, m, volume, ray_weights, row_offsets, measured, shifts):

time: 71.9 us -> 75.7 us (1.053)
  local copies, waits for them, and re-layouts: 5.43 us -> 9.14 us
    unnamed x2 -> x18, local copies, waits for them, and re-layouts: 4.15 us -> 9.14 us
    pallas_call x1, Pallas kernels: 64.6 us -> 62.8 us  [fused(): pl.pallas_call(functools.partial(fit_kernel, n, m), name='fit', out_shape...]
    pallas_call x0 -> x1, Pallas kernels: none -> 1.67 us  [fused(): pl.pallas_call(place_kernel, name='place', out_shape=(jax.ShapeDtypeStruc...]
    slice x1 -> x0, local copies, waits for them, and re-layouts: 1.29 us -> none  [fused(): return (current, residual, slope[:, 0])]
where the time goes in v3:
time: 75.7 us; the launch traced here: 74.2 us
  Pallas kernels  64.5 us (85%)
  local copies, waits for them, and re-layouts  9.14 us (12%)
    pallas_call x1, Pallas kernels, fused(): pl.pallas_call(functools.partial(fit_kernel, n, m), name='fit', out_shape...  62.8 us
    unnamed x18, local copies, waits for them, and re-layouts  9.14 us
    pallas_call x1, Pallas kernels, fused(): pl.pallas_call(place_kernel, name='place', out_shape=(jax.ShapeDtypeStruc...  1.67 us

profile of v3, /device:TPU:1, one launch (start us, length us, event | category | flops | bytes accessed | tf_op | source)
XLA Modules:
  0.0 74.2 jit_solution(6914158286359353702)
XLA Ops:
  0.6 0.0 copy-start
  0.6 2.2 %copy-done = bf16[2,1024,1024]{2,1,0:T(8,128)(2,1)S(1)} copy-done((bf16[2,1024,1024]{2,1,0:T(8,128)(2,1)S(1)}, bf16[2,1024,1024]{2,1,0:T(8,128)(2,1)}, u32[]{:S(2)}) %copy-start) | copy-done | bytes 4194328
  2.8 0.0 copy-start.1
  2.8 1.2 %copy-done.1 = bf16[2,256,1024]{2,1,0:T(8,128)(2,1)S(1)} copy-done((bf16[2,256,1024]{2,1,0:T(8,128)(2,1)S(1)}, bf16[2,256,1024]{2,1,0:T(8,128)(2,1)}, u32[]{:S(2)}) %copy-start.1) | copy-done | bytes 1048600
  4.0 0.0 copy-start.2
  4.0 1.0 %copy-done.2 = f32[2,64,1024]{2,1,0:T(8,128)S(1)} copy-done((f32[2,64,1024]{2,1,0:T(8,128)S(1)}, f32[2,64,1024]{2,1,0:T(8,128)}, u32[]{:S(2)}) %copy-start.2) | copy-done | bytes 524312
  5.1 0.0 copy-start.3
  5.1 0.8 %copy-done.3 = f32[32,512]{1,0:T(8,128)S(1)} copy-done((f32[32,512]{1,0:T(8,128)S(1)}, f32[32,512]{1,0:T(8,128)}, u32[]{:S(2)}) %copy-start.3) | copy-done | bytes 65560
  5.9 0.0 copy-start.4
  5.9 0.8 %copy-done.4 = f32[32,512]{1,0:T(8,128)S(1)} copy-done((f32[32,512]{1,0:T(8,128)S(1)}, f32[32,512]{1,0:T(8,128)}, u32[]{:S(2)}) %copy-start.4) | copy-done | bytes 65560
  6.8 0.0 copy-start.5
  6.8 0.8 %copy-done.5 = f32[32,512]{1,0:T(8,128)S(1)} copy-done((f32[32,512]{1,0:T(8,128)S(1)}, f32[32,512]{1,0:T(8,128)}, u32[]{:S(2)}) %copy-start.5) | copy-done | bytes 65560
  7.6 0.0 copy-start.6
  7.6 0.8 %copy-done.6 = f32[32,512]{1,0:T(8,128)S(1)} copy-done((f32[32,512]{1,0:T(8,128)S(1)}, f32[32,512]{1,0:T(8,128)}, u32[]{:S(2)}) %copy-start.6) | copy-done | bytes 65560
  8.4 0.0 copy-start.7
  8.4 0.7 copy-done.7
  9.1 0.0 copy-start.8
  9.1 0.7 copy-done.8
  9.8 62.8 %fit.1 = (bf16[2,256,1024]{2,1,0:T(8,128)(2,1)S(1)}, f32[2,64,1024]{2,1,0:T(8,128)S(1)}, f32[2,128]{1,0:T(2,128)S(1)}) custom-call(s32[2,8]{1,0:T(2,128)S(1)} %copy-done.7, f32[2]{0:T(128)S(1)} %copy-done.8, bf16[2,256,1024]{2,1,0:T(8,128)(2,1)S(1)} %copy-done.1, bf16[2,1024,1024]{2,1,0:T(8,128)(2,1)S(1)} %copy-done, f32[2,64,1024]{2,1,0:T(8,128)S(1)} %copy-done.2, ...), custom_call_target="tpu_custom_call" | custom-call | tf_op jit(solution)/shard_map/fit/pallas_call | solution.py:566
  72.6 1.7 %place.1 = (bf16[2,256,1024]{2,1,0:T(8,128)(2,1)}, f32[2,64,1024]{2,1,0:T(8,128)}, f32[2]{0:T(128)}) custom-call(bf16[2,256,1024]{2,1,0:T(8,128)(2,1)S(1)} %get-tuple-element.6.current, f32[2,64,1024]{2,1,0:T(8,128)S(1)} %get-tuple-element.7.residual, f32[2,128]{1,0:T(2,128)S(1)} %get-tuple-element.8.slope), custom_call_target="tpu_custom_call" | custom-call | tf_op jit(solution)/shard_map/place/pallas_call | solution.py:615
Async XLA Ops:
  0.6 2.2 %copy-start = (bf16[2,1024,1024]{2,1,0:T(8,128)(2,1)S(1)}, bf16[2,1024,1024]{2,1,0:T(8,128)(2,1)}, u32[]{:S(2)}) copy-start(bf16[2,1024,1024]{2,1,0:T(8,128)(2,1)} %w_hbm.1) | copy-start | bytes 12582916
  2.8 1.2 %copy-start.1 = (bf16[2,256,1024]{2,1,0:T(8,128)(2,1)S(1)}, bf16[2,256,1024]{2,1,0:T(8,128)(2,1)}, u32[]{:S(2)}) copy-start(bf16[2,256,1024]{2,1,0:T(8,128)(2,1)} %vol.1) | copy-start | bytes 3145732
  4.0 1.0 %copy-start.2 = (f32[2,64,1024]{2,1,0:T(8,128)S(1)}, f32[2,64,1024]{2,1,0:T(8,128)}, u32[]{:S(2)}) copy-start(f32[2,64,1024]{2,1,0:T(8,128)} %meas.1) | copy-start | bytes 1572868
  5.1 0.8 %copy-start.3 = (f32[32,512]{1,0:T(8,128)S(1)}, f32[32,512]{1,0:T(8,128)}, u32[]{:S(2)}) copy-start(f32[32,512]{1,0:T(8,128)} %constant.11.clone.gtab) | copy-start | bytes 196612
  5.9 0.8 %copy-start.4 = (f32[32,512]{1,0:T(8,128)S(1)}, f32[32,512]{1,0:T(8,128)}, u32[]{:S(2)}) copy-start(f32[32,512]{1,0:T(8,128)} %constant.10.clone.ftab) | copy-start | bytes 196612
  6.8 0.8 %copy-start.5 = (f32[32,512]{1,0:T(8,128)S(1)}, f32[32,512]{1,0:T(8,128)}, u32[]{:S(2)}) copy-start(f32[32,512]{1,0:T(8,128)} %constant.9.clone.stab) | copy-start | bytes 196612
  7.6 0.8 %copy-start.6 = (f32[32,512]{1,0:T(8,128)S(1)}, f32[32,512]{1,0:T(8,128)}, u32[]{:S(2)}) copy-start(f32[32,512]{1,0:T(8,128)} %constant.8.clone.ctab) | copy-start | bytes 196612
  8.4 0.7 copy-start.7
  9.1 0.7 copy-start.8
